TPU v7x, 256 devices: a whole 4x4x8 slice. The times are simulated.
256 devices in a mesh: row: 16 (over z, y_hi), col: 16 (over y_lo, x, core).
Axes of the slice: x: 4, y: 4 (y_hi: 2, y_lo: 2; y = y_hi * 2 + y_lo), z: 8, core: 2. Of those that a mesh axis runs over, the one named last changes fastest.
Arguments:
- object_slab: float32 [2, 5120, 5120], P(None, 'row', 'col'), may hold values from -5 to 5
- probe_field: float32 [2, 512, 512], replicated, may hold values from -5 to 5
- offsets: int32 [16, 16, 1, 2], P('row', 'col'), may hold values from 0 to 64
- counts: int32 [16, 16, 1, 512, 512], P('row', 'col'), may hold values from 0 to 399
Outputs:
- updated: float32 [2, 5120, 5120], P(None, 'row', 'col')
Inputs may be any that keep to these rules, and one draw needn't show every extreme that they name: Window offsets inside the widened tile of 576 cells a side; the window never leaves it.
All inputs are finite; a program needn't handle non-finite values.
Results may differ from a plain program's by a relative error of at most 0.0003.
Values sent between devices are 32-bit elements; how exact they have to be, the bound alone decides.
A program may use at most 128 MiB of HBM per device.

v0:
```python
import functools
import math

import jax
import jax.numpy as jnp
import numpy as np
from jax import lax
from jax.experimental import pallas as pl
from jax.experimental.pallas import tpu as pltpu
from jax.sharding import PartitionSpec as P

EPSILON = 0.01
PHOTON_SCALE = 0.01
STEP_SIZE = 0.5
REGULAR = 1.0

N = 512
B = 128
OWN = 320
NOWHERE = -10000.0
F32 = jnp.float32
BF16 = jnp.bfloat16
POS = (1, 2, 3, 0)


def tables():
    k = np.arange(B)[:, None]
    n = np.arange(B)[None, :]
    out = []
    for r in range(4):
        angle = 2.0 * math.pi * (((4 * k + r) * n) % N) / N
        c, s = np.cos(angle) / math.sqrt(N), np.sin(angle) / math.sqrt(N)
        out.append(np.block([[c, s], [-s, c]]))
    full = np.stack(out).astype(np.float32)
    both = np.stack([full, full.transpose(0, 2, 1)])
    high = both.astype(jnp.bfloat16)
    low = (both - high.astype(np.float32)).astype(jnp.bfloat16)
    return np.stack([high, low])


def split(x):
    high = x.astype(BF16)
    return high, (x - high.astype(F32)).astype(BF16)


def dot(a, b):
    return jnp.dot(a, b, preferred_element_type=F32)


def iota(shape, dim):
    return lax.broadcasted_iota(jnp.int32, shape, dim)


def onehot(mask):
    return jnp.where(mask, 1.0, 0.0).astype(BF16)


def roll64(x):
    return pltpu.roll(x, 64, 1)


def kernel(
    rows, cols,
    obj_hbm, probe_hbm, off_ref, counts_hbm, tab_hbm,
    out_ref,
    obj, probe, counts, tab, offs, edge, mid_up, mid_dn,
    in_edge, in_mid, in_own, in_cor,
    lum, pp, meas, light, ex, zh, zl, y, kh, kl, w, acc, g, sg, rg, s_edge, s_mid, r_edge, r_mid,
    load_sem, send_sem, recv_sem,
):
    row, col = lax.axis_index("row"), lax.axis_index("col")
    has = (row > 0, row < rows - 1, col > 0, col < cols - 1)
    peer = ({"row": row - 1}, {"row": row + 1}, {"col": col - 1}, {"col": col + 1})
    UP, DN, LF, RT = range(4)
    MESH = pl.DeviceIdType.MESH

    def load(src, dst, i):
        return pltpu.make_async_copy(src, dst, load_sem.at[i])

    loads = [
        load(obj_hbm, obj, 0),
        load(probe_hbm, probe, 1),
        load(counts_hbm.at[0, 0, 0], counts, 2),
        load(tab_hbm, tab, 3),
    ]
    for c in loads:
        c.start()

    barrier = pltpu.get_barrier_semaphore()
    for d in range(4):
        @pl.when(has[d])
        def _():
            pl.semaphore_signal(barrier, inc=1, device_id=peer[d], device_id_type=MESH)

    def message(direction, slot, src, dst):
        return pltpu.make_async_remote_copy(
            src_ref=src, dst_ref=dst,
            send_sem=send_sem.at[slot], recv_sem=recv_sem.at[slot],
            device_id=peer[direction], device_id_type=MESH,
        )

    def send(direction, slot, src, dst):
        @pl.when(has[direction])
        def _():
            message(direction, slot, src, dst).start()

    OPP = (DN, UP, RT, LF)
    plan = {
        ("off", UP): (0, offs.at[1, 1], offs.at[1, 2]),
        ("off", DN): (1, offs.at[1, 1], offs.at[1, 0]),
        ("edge", UP): (2, edge.at[:, :, 0:B], in_edge.at[1]),
        ("edge", DN): (3, edge.at[:, :, OWN - B:OWN], in_edge.at[0]),
        ("mid", UP): (4, mid_up, in_mid.at[1]),
        ("mid", DN): (5, mid_dn, in_mid.at[0]),
        ("off", LF): (6, offs.at[1], offs.at[2]),
        ("off", RT): (7, offs.at[1], offs.at[0]),
        ("own", LF): (8, edge.at[0], in_own.at[1]),
        ("own", RT): (9, edge.at[1], in_own.at[0]),
        ("cor0", LF): (10, in_edge.at[0, 0], in_cor.at[1, 0]),
        ("cor0", RT): (11, in_edge.at[0, 1], in_cor.at[0, 0]),
        ("cor1", LF): (12, in_edge.at[1, 0], in_cor.at[1, 1]),
        ("cor1", RT): (13, in_edge.at[1, 1], in_cor.at[0, 1]),
        ("gcor", LF): (14, sg.at[0, :, 0:192], rg.at[1, :, 0:192]),
        ("gcor", RT): (15, sg.at[1, :, 0:192], rg.at[0, :, 0:192]),
        ("gown", LF): (16, sg.at[0, :, 192:N], rg.at[1, :, 192:N]),
        ("gown", RT): (17, sg.at[1, :, 192:N], rg.at[0, :, 192:N]),
        ("gmid", UP): (18, s_mid.at[0], r_mid.at[1]),
        ("gmid", DN): (19, s_mid.at[1], r_mid.at[0]),
        ("gedge", UP): (20, s_edge.at[0], r_edge.at[1]),
        ("gedge", DN): (21, s_edge.at[1], r_edge.at[0]),
    }

    def go(name, direction):
        send(direction, *plan[name, direction])

    def arrive(name, side):
        slot, src, dst = plan[name, OPP[side]]

        @pl.when(has[side])
        def _():
            message(side, slot, src, dst).wait_recv()

    u, v = off_ref[0, 0, 0, 0], off_ref[0, 0, 0, 1]
    lane_row = lambda n: iota((n, B), 1)
    low_half = lane_row(64) < 64

    @pl.when(row == 0)
    def _():
        in_edge[0] = jnp.zeros(in_edge.shape[1:], F32)
        in_mid[0] = jnp.zeros(in_mid.shape[1:], F32)
        r_edge[0] = jnp.zeros(r_edge.shape[1:], F32)
        r_mid[0] = jnp.zeros(r_mid.shape[1:], F32)
        offs[1, 0] = jnp.full((8, B), NOWHERE, F32)

    @pl.when(row == rows - 1)
    def _():
        in_edge[1] = jnp.zeros(in_edge.shape[1:], F32)
        in_mid[1] = jnp.zeros(in_mid.shape[1:], F32)
        r_edge[1] = jnp.zeros(r_edge.shape[1:], F32)
        r_mid[1] = jnp.zeros(r_mid.shape[1:], F32)
        offs[1, 2] = jnp.full((8, B), NOWHERE, F32)

    @pl.when(col == 0)
    def _():
        in_own[0] = jnp.zeros(in_own.shape[1:], F32)
        in_cor[0] = jnp.zeros(in_cor.shape[1:], F32)
        rg[0] = jnp.zeros(rg.shape[1:], F32)
        offs[0] = jnp.full((3, 8, B), NOWHERE, F32)

    @pl.when(col == cols - 1)
    def _():
        in_own[1] = jnp.zeros(in_own.shape[1:], F32)
        in_cor[1] = jnp.zeros(in_cor.shape[1:], F32)
        rg[1] = jnp.zeros(rg.shape[1:], F32)
        offs[2] = jnp.full((3, 8, B), NOWHERE, F32)

    uf, vf = u.astype(F32), v.astype(F32)
    offs[1, 1] = jnp.where(iota((8, B), 0) == 0, uf, vf)

    loads[0].wait()
    def tail(rs, n, ch):
        x = obj[ch, rs:rs + n, 256:OWN]
        return jnp.concatenate([x, x], axis=1)

    for ch in range(2):
        edge[0, ch] = obj[ch, :, 0:B]
        edge[1, ch] = jnp.where(
            lane_row(OWN) < 64, roll64(obj[ch, :, B:256]), tail(0, OWN, ch)
        )
    for ref, rs in ((mid_up, 0), (mid_dn, OWN - B)):
        ref[...] = jnp.where(
            lane_row(B) < 64, obj[0, rs:rs + B, B:256], roll64(obj[1, rs:rs + B, B:256])
        )

    pl.semaphore_wait(
        barrier,
        sum(h.astype(jnp.int32) for h in has),
    )

    for name in ("off", "edge", "mid"):
        go(name, UP)
        go(name, DN)
    go("own", LF)
    go("own", RT)

    loads[1].wait()
    for q in range(4):
        rs = slice(q * B, (q + 1) * B)
        pr, pi = probe[0, rs], probe[1, rs]
        hi, lo = split(pr * pr + pi * pi)
        lum[0, rs] = hi
        lum[1, rs] = lo
    d = iota((N, N), 0) + v - ((iota((N, N), 1) + 3 * B) % N)
    right = onehot((d == 0) | (d == N))
    d = iota((N, N), 1) + u - iota((N, N), 0)
    left = onehot((d == 0) | (d == N))
    for ch in range(2):
        hi, lo = split(probe[ch])
        hi, lo = split(dot(hi, right) + dot(lo, right))
        pp[ch] = dot(left, hi) + dot(left, lo)

    arrive("off", UP)
    arrive("off", DN)
    go("off", LF)
    go("off", RT)

    loads[2].wait()
    a, b = iota((N, N), 0), iota((N, N), 1)
    order_right = onehot(a == (b % B) * 4 + b // B)
    order_left = onehot(b == (a % B) * 4 + a // B)
    hi, lo = split(counts[...].astype(F32))
    hi, lo = split(dot(hi, order_right) + dot(lo, order_right))
    meas[...] = jnp.sqrt((dot(order_left, hi) + dot(order_left, lo)) * PHOTON_SCALE)

    arrive("off", LF)
    arrive("off", RT)
    light[...] = jnp.zeros(light.shape, F32)
    row_of = ((0, B, 384, B, 448), (0, OWN, 0, N, 128), (192, B, 0, B, -192))
    col_of = ((0, B, 384, B, 448), (0, 384, 0, N, 128), (128, 256, 0, B, -192))

    def tiled(x, n):
        return x if n == B else jnp.concatenate([x] * (n // B), axis=1)

    for dc in range(3):
        c0, cn, j0, jn, cshift = col_of[dc]
        for dr in range(3):
            r0, rn, i0, im, rshift = row_of[dr]
            ou = tiled(offs[dc, dr, 0:1, :], im)
            ov = tiled(offs[dc, dr, 1:2, :], cn)
            i_row = (iota((rn, im), 1) + (i0 - r0 - rshift) - iota((rn, im), 0)).astype(F32)
            pick_row = onehot(i_row + ou == 0.0)
            i_col = (iota((jn, cn), 0) + (j0 - c0 - cshift) - iota((jn, cn), 1)).astype(F32)
            pick_col = onehot(i_col + ov == 0.0)
            part = sum(dot(pick_row, lum[h, i0:i0 + im, j0:j0 + jn]) for h in range(2))
            hi, lo = split(part)
            light[r0:r0 + rn, c0:c0 + cn] += dot(hi, pick_col) + dot(lo, pick_col)
    light[...] = STEP_SIZE / (light[...] + REGULAR)

    def put(rs, n, t, wr, wi):
        at = (slice(rs, rs + n), slice(POS[t] * B, (POS[t] + 1) * B))
        pr, pi = pp[(0,) + at], pp[(1,) + at]
        ex[(0,) + at] = pr * wr - pi * wi
        ex[(1,) + at] = pr * wi + pi * wr

    arrive("own", LF)
    arrive("own", RT)
    put(B, OWN, 1, obj[0, :, 0:B], obj[1, :, 0:B])
    put(B, OWN, 2, obj[0, :, B:256], obj[1, :, B:256])

    def side_tiles(rs, n, ends, from_left, from_right):
        half = lane_row(n) < 64
        back = [roll64(x) for x in from_right]
        put(rs, n, 3, *(jnp.where(half, e, x) for e, x in zip(ends, back)))
        put(rs, n, 0, *(jnp.where(lane_row(n) < v, x, y_) for x, y_ in zip(back, from_left)))

    side_tiles(
        B, OWN, [tail(0, OWN, ch) for ch in range(2)],
        [in_own[0, ch] for ch in range(2)], [in_own[1, ch] for ch in range(2)],
    )

    loads[3].wait()
    for side in (UP, DN):
        arrive("edge", side)
        go("cor%d" % side, LF)
        go("cor%d" % side, RT)
    arrive("mid", UP)
    arrive("mid", DN)

    groups = (0, 64, 448)
    row64 = iota((64, B), 0)

    def halo(group, get):
        if group == 0:
            return jnp.where(row64 < u, get(1, 64), get(0, 0))
        if group == 64:
            return get(0, 64)
        return get(1, 0)

    def rolled_edge(group, ch):
        return roll64(halo(group, lambda s, r: in_edge[s, 1, ch, r:r + 64]))

    for rs in groups:
        put(rs, 64, 1, *(halo(rs, lambda s, r: in_edge[s, 0, ch, r:r + 64]) for ch in range(2)))
        m = halo(rs, lambda s, r: in_mid[s, r:r + 64])
        put(rs, 64, 2, *(
            jnp.where(low_half, m if ch == 0 else roll64(m), rolled_edge(rs, ch))
            for ch in range(2)
        ))

    def fwd4(x):
        (ar, ai), (br, bi), (cr, ci), (dr_, di) = x
        er, ei, fr, fi = ar + cr, ai + ci, ar - cr, ai - ci
        gr, gi, hr, hi_ = br + dr_, bi + di, br - dr_, bi - di
        return [
            (er + gr, ei + gi), (fr + hi_, fi - hr),
            (er - gr, ei - gi), (fr - hi_, fi + hr),
        ]

    def inv4(x):
        (ar, ai), (br, bi), (cr, ci), (dr_, di) = x
        er, ei, fr, fi = ar + cr, ai + ci, ar - cr, ai - ci
        gr, gi, hr, hi_ = br + dr_, bi + di, br - dr_, bi - di
        return [
            (er + gr, ei + gi), (fr - hi_, fi + hr),
            (er - gr, ei - gi), (fr + hi_, fi - hr),
        ]

    def stage_left_in(p):
        ls = slice(p * 256, p * 256 + 256)
        z = fwd4([(ex[0, q * B:(q + 1) * B, ls], ex[1, q * B:(q + 1) * B, ls]) for q in range(4)])
        for r in range(4):
            for c in range(2):
                hi, lo = split(z[r][c])
                zh[r, c * B:(c + 1) * B, ls] = hi
                zl[r, c * B:(c + 1) * B, ls] = lo
        for r in range(4):
            y[r, :, ls] = (
                dot(tab[0, 0, r], zh[r, :, ls])
                + dot(tab[0, 0, r], zl[r, :, ls])
                + dot(tab[1, 0, r], zh[r, :, ls])
            )

    stage_left_in(1)
    for side in (UP, DN):
        arrive("cor%d" % side, LF)
        arrive("cor%d" % side, RT)
    for rs in groups:
        side_tiles(
            rs, 64, [rolled_edge(rs, ch) for ch in range(2)],
            [halo(rs, lambda s, r: in_cor[0, s, ch, r:r + 64]) for ch in range(2)],
            [halo(rs, lambda s, r: in_cor[1, s, ch, r:r + 64]) for ch in range(2)],
        )
    stage_left_in(0)

    def dot3(a_hi, a_lo, b_hi, b_lo):
        return dot(a_hi, b_hi) + dot(a_hi, b_lo) + dot(a_lo, b_hi)

    for r in range(4):
        z = fwd4([
            tuple(y[r, c * B:(c + 1) * B, POS[q] * B:(POS[q] + 1) * B] for c in range(2))
            for q in range(4)
        ])
        for s in range(4):
            for c in range(2):
                hi, lo = split(z[s][c])
                kh[s, r * B:(r + 1) * B, c * B:(c + 1) * B] = hi
                kl[s, r * B:(r + 1) * B, c * B:(c + 1) * B] = lo
    for s in range(4):
        far = dot3(kh[s], kl[s], tab[0, 1, s], tab[1, 1, s])
        fr, fi = far[:, 0:B], far[:, B:256]
        factor = 1.0 - meas[:, s * B:(s + 1) * B] * lax.rsqrt(fr * fr + fi * fi + EPSILON)
        hi, lo = split(jnp.concatenate([factor * fr, factor * fi], axis=1))
        w[s] = dot3(hi, lo, tab[0, 0, s], tab[1, 0, s])

    for r in range(4):
        rs = slice(r * B, (r + 1) * B)
        x = inv4([(w[s, rs, 0:B], w[s, rs, B:256]) for s in range(4)])
        for q in range(4):
            for c in range(2):
                hi, lo = split(x[q][c])
                zh[r, c * B:(c + 1) * B, POS[q] * B:(POS[q] + 1) * B] = hi
                zl[r, c * B:(c + 1) * B, POS[q] * B:(POS[q] + 1) * B] = lo

    def stage_left_out(p):
        ls = slice(p * 256, p * 256 + 256)
        for r in range(4):
            y[r, :, ls] = (
                dot(tab[0, 1, r], zh[r, :, ls])
                + dot(tab[0, 1, r], zl[r, :, ls])
                + dot(tab[1, 1, r], zh[r, :, ls])
            )
        x = inv4([(y[r, 0:B, ls], y[r, B:256, ls]) for r in range(4)])
        for q in range(4):
            rs = slice(q * B, (q + 1) * B)
            pr, pi = pp[0, rs, ls], pp[1, rs, ls]
            br, bi = x[q]
            g[0, rs, ls] = pr * br + pi * bi
            g[1, rs, ls] = pr * bi - pi * br

    stage_left_out(0)
    for rs, n, m in ((448, 64, 0), (0, 448, 64)):
        lanes = lane_row(n)
        for c in range(2):
            g3, g0 = g[c, rs:rs + n, 0:B], g[c, rs:rs + n, B:256]
            inner = lanes < v
            sg[0, c, m:m + n] = jnp.where(inner, 0.0, g0)
            sg[1, c, m:m + n] = roll64(jnp.where(lanes >= 64, g3, jnp.where(inner, g0, 0.0)))
    for name in ("gcor", "gown"):
        go(name, LF)
        go(name, RT)
    stage_left_out(1)

    row64f = row64.astype(F32)

    def outgoing(side, get, ou):
        if side == UP:
            return (jnp.where(row64f >= ou, get(0), 0.0), get(64))
        return (get(448), jnp.where(row64f < ou, get(0), 0.0))

    own_u = offs[1, 1, 0:1, :]

    def tile(c, rs, n, t):
        return g[c, rs:rs + n, POS[t] * B:(POS[t] + 1) * B]

    for side in (UP, DN):
        m = outgoing(
            side,
            lambda rs: jnp.where(low_half, tile(0, rs, 64, 2), roll64(tile(1, rs, 64, 2))),
            own_u,
        )
        for h in range(2):
            s_mid[side, h * 64:h * 64 + 64] = m[h]
        go("gmid", side)
    arrive("gcor", LF)
    arrive("gcor", RT)
    for side in (UP, DN):
        for c in range(2):
            mine = (
                lambda rs: tile(c, rs, 64, 1),
                lambda rs: roll64(jnp.where(low_half, tile(c, rs, 64, 3), tile(c, rs, 64, 2))),
            )
            for e in range(2):
                m = outgoing(side, mine[e], own_u)
                o = outgoing(
                    side,
                    lambda rs: rg[e, c, (rs + 64) % N:(rs + 64) % N + 64],
                    offs[2 * e, 1, 0:1, :],
                )
                for h in range(2):
                    s_edge[side, e, c, h * 64:h * 64 + 64] = m[h] + o[h]
        go("gedge", side)

    arrive("gown", LF)
    arrive("gown", RT)
    lanes = lane_row(OWN)
    for c in range(2):
        x = roll64(rg[1, c, 192:N])
        acc[c, :, 0:B] = light[:, 0:B] * (tile(c, B, OWN, 1) + rg[0, c, 192:N])
        acc[c, :, B:256] = light[:, B:256] * (
            tile(c, B, OWN, 2) + jnp.where(lanes >= 64, x, 0.0)
        )
        acc[c, :, 256:384] = light[:, 256:384] * (tile(c, B, OWN, 3) + x)
        out_ref[c, B:192, :] = acc[c, B:192, 0:OWN]

    for side, rs in ((UP, 0), (DN, 192)):
        arrive("gmid", side)
        arrive("gedge", side)
        at = slice(rs, rs + B)
        for c in range(2):
            x = roll64(r_edge[side, 1, c])
            m = r_mid[side] if c == 0 else roll64(r_mid[side])
            out_ref[c, at, 0:B] = acc[c, at, 0:B] + light[at, 0:B] * r_edge[side, 0, c]
            out_ref[c, at, B:256] = acc[c, at, B:256] + light[at, B:256] * jnp.where(
                lane_row(B) < 64, m, x
            )
            last = acc[c, at, 256:384] + light[at, 256:384] * x
            out_ref[c, at, 256:OWN] = last[:, 0:64]

    for (name, direction), (slot, src, dst) in plan.items():
        @pl.when(has[direction])
        def _():
            message(direction, slot, src, dst).wait_send()


def local(rows, cols, object_slab, probe_field, offsets, counts):
    hbm = pl.BlockSpec(memory_space=pl.ANY)
    vmem = pltpu.VMEM
    step = pl.pallas_call(
        functools.partial(kernel, rows, cols),
        out_shape=jax.ShapeDtypeStruct((2, OWN, OWN), F32),
        in_specs=[hbm, hbm, pl.BlockSpec(memory_space=pltpu.SMEM), hbm, hbm],
        out_specs=pl.BlockSpec(memory_space=pltpu.VMEM),
        scratch_shapes=[
            vmem((2, OWN, OWN), F32),
            vmem((2, N, N), F32),
            vmem((N, N), jnp.int32),
            vmem((2, 2, 4, 256, 256), BF16),
            vmem((3, 3, 8, B), F32),
            vmem((2, 2, OWN, B), F32),
            vmem((B, B), F32),
            vmem((B, B), F32),
            vmem((2, 2, 2, B, B), F32),
            vmem((2, B, B), F32),
            vmem((2, 2, OWN, B), F32),
            vmem((2, 2, 2, B, B), F32),
            vmem((2, N, N), BF16),
            vmem((2, N, N), F32),
            vmem((N, N), F32),
            vmem((OWN, 384), F32),
            vmem((2, N, N), F32),
            vmem((4, 256, N), BF16),
            vmem((4, 256, N), BF16),
            vmem((4, 256, N), F32),
            vmem((4, N, 256), BF16),
            vmem((4, N, 256), BF16),
            vmem((4, N, 256), F32),
            vmem((2, OWN, 384), F32),
            vmem((2, N, N), F32),
            vmem((2, 2, N, B), F32),
            vmem((2, 2, N, B), F32),
            vmem((2, 2, 2, B, B), F32),
            vmem((2, B, B), F32),
            vmem((2, 2, 2, B, B), F32),
            vmem((2, B, B), F32),
            pltpu.SemaphoreType.DMA((4,)),
            pltpu.SemaphoreType.DMA((22,)),
            pltpu.SemaphoreType.DMA((22,)),
        ],
        compiler_params=pltpu.CompilerParams(
            collective_id=0, has_side_effects=True, vmem_limit_bytes=56 * 1024 * 1024
        ),
        name="step",
    )
    return object_slab - step(
        object_slab, probe_field, offsets, counts, jnp.asarray(tables())
    )


def solution(mesh):
    return jax.shard_map(
        functools.partial(local, mesh.shape["row"], mesh.shape["col"]),
        mesh=mesh,
        in_specs=(
            P(None, "row", "col"),
            P(),
            P("row", "col", None, None),
            P("row", "col", None, None, None),
        ),
        out_specs=P(None, "row", "col"),
        check_vma=False,
    )
```

profile of v0, /device:TPU:161, one launch (start us, length us, event | category | flops | bytes accessed | tf_op | source)
XLA Modules:
  0.0 56.6 jit_solution(2095005254775622013)
XLA Ops:
  0.0 0.0 copy-start
  0.0 54.3 %step.1 = f32[2,320,320]{2,1,0:T(8,128)} custom-call(f32[2,320,320]{2,1,0:T(8,128)} %obj_hbm.1, f32[2,512,512]{2,1,0:T(8,128)} %probe_hbm.1, s32[1,1,1,2]{3,2,1,0:T(1,128)} %off_ref.1, s32[1,1,1,512,512]{4,3,2,1,0:T(8,128)} %counts_hbm.1, bf16[2,2,4,256,256]{4,3,2,1,0:T(8,128)(2,1)} %constant.2.clone.tab_hbm), custom_call_target="tpu_custom_call" | custom-call | tf_op jit(solution)/shard_map/step/pallas_call | solution.py:534
  54.4 0.0 copy-done
  54.4 2.2 %sub.3 = f32[2,320,320]{2,1,0:T(8,128)} subtract(f32[2,320,320]{2,1,0:T(8,128)S(1)} %copy-done, f32[2,320,320]{2,1,0:T(8,128)} %step.1) | non-fusion elementwise | flops 204800 | bytes 2457600 | tf_op jit(solution)/shard_map/sub | solution.py:534
Async XLA Ops:
  0.0 54.4 %copy-start = (f32[2,320,320]{2,1,0:T(8,128)S(1)}, f32[2,320,320]{2,1,0:T(8,128)}, u32[]{:S(2)}) copy-start(f32[2,320,320]{2,1,0:T(8,128)} %obj_hbm.1) | copy-start | bytes 2457604
where the time goes:
time: 57.6 us; the launch traced here: 56.6 us
  Pallas kernels  54.3 us (94%)
  other arithmetic  2.25 us (4%)
    pallas_call x1, Pallas kernels, local(): step(object_slab, probe_field, offsets, counts, jnp.asarray(tables()))  54.3 us
    sub x1, other arithmetic, local(): object_slab - step(object_slab, probe_field, offsets, counts, jnp.asarray...  2.25 us

commit v1 on v0

--- a/solution.py
+++ b/solution.py
@@ -64,11 +64,12 @@
     obj_hbm, probe_hbm, off_ref, counts_hbm, tab_hbm,
     out_ref,
     obj, probe, counts, tab, offs, edge, mid_up, mid_dn,
-    in_edge, in_mid, in_own, in_cor,
+    in_edge, in_mid, in_own, in_cor, relay_in,
     lum, pp, meas, light, ex, zh, zl, y, kh, kl, w, acc, g, sg, rg, s_edge, s_mid, r_edge, r_mid,
     load_sem, send_sem, recv_sem,
 ):
     row, col = lax.axis_index("row"), lax.axis_index("col")
+    core = lax.rem(col, 2)
     has = (row > 0, row < rows - 1, col > 0, col < cols - 1)
     peer = ({"row": row - 1}, {"row": row + 1}, {"col": col - 1}, {"col": col + 1})
     UP, DN, LF, RT = range(4)
@@ -92,6 +93,24 @@
         def _():
             pl.semaphore_signal(barrier, inc=1, device_id=peer[d], device_id_type=MESH)
 
+    OPP = (DN, UP, RT, LF)
+    CROSS = (8, 7)
+    RELAYS = {LF: (5, 3), RT: (11, 13)}
+    RELAYED = ("own0", "own1", "gown0", "gown1")
+    crossers = [(col == c) for c in CROSS]
+    is_relay = functools.reduce(
+        jnp.logical_or, [col == c for d in (LF, RT) for c in RELAYS[d]]
+    )
+    @pl.when(is_relay)
+    def _():
+        for c in CROSS:
+            pl.semaphore_signal(barrier, inc=1, device_id={"col": c}, device_id_type=MESH)
+
+    @pl.when(functools.reduce(jnp.logical_or, crossers))
+    def _():
+        for c in RELAYS[LF] + RELAYS[RT]:
+            pl.semaphore_signal(barrier, inc=1, device_id={"col": c}, device_id_type=MESH)
+
     def message(direction, slot, src, dst):
         return pltpu.make_async_remote_copy(
             src_ref=src, dst_ref=dst,
@@ -104,34 +123,77 @@
         def _():
             message(direction, slot, src, dst).start()
 
-    OPP = (DN, UP, RT, LF)
     plan = {
         ("off", UP): (0, offs.at[1, 1], offs.at[1, 2]),
         ("off", DN): (1, offs.at[1, 1], offs.at[1, 0]),
-        ("edge", UP): (2, edge.at[:, :, 0:B], in_edge.at[1]),
-        ("edge", DN): (3, edge.at[:, :, OWN - B:OWN], in_edge.at[0]),
+        ("outer", UP): (2, edge.at[core, :, 0:B], in_edge.at[1, core]),
+        ("outer", DN): (3, edge.at[core, :, OWN - B:OWN], in_edge.at[0, core]),
+        ("inner", UP): (28, edge.at[1 - core, :, 0:B], in_edge.at[1, 1 - core]),
+        ("inner", DN): (29, edge.at[1 - core, :, OWN - B:OWN], in_edge.at[0, 1 - core]),
         ("mid", UP): (4, mid_up, in_mid.at[1]),
         ("mid", DN): (5, mid_dn, in_mid.at[0]),
         ("off", LF): (6, offs.at[1], offs.at[2]),
         ("off", RT): (7, offs.at[1], offs.at[0]),
-        ("own", LF): (8, edge.at[0], in_own.at[1]),
-        ("own", RT): (9, edge.at[1], in_own.at[0]),
+        ("own0", LF): (8, edge.at[0, :, 0:160], in_own.at[1, :, 0:160]),
+        ("own0", RT): (9, edge.at[1, :, 0:160], in_own.at[0, :, 0:160]),
+        ("own1", LF): (22, edge.at[0, :, 160:OWN], in_own.at[1, :, 160:OWN]),
+        ("own1", RT): (23, edge.at[1, :, 160:OWN], in_own.at[0, :, 160:OWN]),
         ("cor0", LF): (10, in_edge.at[0, 0], in_cor.at[1, 0]),
         ("cor0", RT): (11, in_edge.at[0, 1], in_cor.at[0, 0]),
         ("cor1", LF): (12, in_edge.at[1, 0], in_cor.at[1, 1]),
         ("cor1", RT): (13, in_edge.at[1, 1], in_cor.at[0, 1]),
         ("gcor", LF): (14, sg.at[0, :, 0:192], rg.at[1, :, 0:192]),
         ("gcor", RT): (15, sg.at[1, :, 0:192], rg.at[0, :, 0:192]),
-        ("gown", LF): (16, sg.at[0, :, 192:N], rg.at[1, :, 192:N]),
-        ("gown", RT): (17, sg.at[1, :, 192:N], rg.at[0, :, 192:N]),
+        ("gown0", LF): (16, sg.at[0, :, 192:352], rg.at[1, :, 192:352]),
+        ("gown0", RT): (17, sg.at[1, :, 192:352], rg.at[0, :, 192:352]),
+        ("gown1", LF): (24, sg.at[0, :, 352:N], rg.at[1, :, 352:N]),
+        ("gown1", RT): (25, sg.at[1, :, 352:N], rg.at[0, :, 352:N]),
         ("gmid", UP): (18, s_mid.at[0], r_mid.at[1]),
         ("gmid", DN): (19, s_mid.at[1], r_mid.at[0]),
         ("gedge", UP): (20, s_edge.at[0], r_edge.at[1]),
         ("gedge", DN): (21, s_edge.at[1], r_edge.at[0]),
     }
 
+    def routed(name, direction):
+        slot, src, dst = plan[name, direction]
+        k, held, held_slot = {
+            "own0": (0, relay_in.at[0], 26), "own1": (1, relay_in.at[0], 26),
+            "gown0": (0, relay_in.at[1], 27), "gown1": (1, relay_in.at[1], 27),
+        }[name]
+
+        def leg(source, target, sent, received, to):
+            return pltpu.make_async_remote_copy(
+                src_ref=source, dst_ref=target,
+                send_sem=send_sem.at[sent], recv_sem=recv_sem.at[received],
+                device_id={"col": to}, device_id_type=MESH,
+            )
+
+        via, end = RELAYS[direction][k], CROSS[1 - (direction - LF)]
+        return via, leg(src, held, slot, held_slot, via), leg(held, dst, held_slot, slot, end)
+
     def go(name, direction):
-        send(direction, *plan[name, direction])
+        if direction not in (LF, RT) or name not in RELAYED:
+            send(direction, *plan[name, direction])
+            return
+        crossing = col == CROSS[direction - LF]
+
+        @pl.when(has[direction] & jnp.logical_not(crossing))
+        def _():
+            message(direction, *plan[name, direction]).start()
+
+        @pl.when(crossing)
+        def _():
+            routed(name, direction)[1].start()
+
+    def pass_on(*names):
+        for name in names:
+            for direction in (LF, RT):
+                via, first, second = routed(name, direction)
+
+                @pl.when(col == via)
+                def _():
+                    first.wait_recv()
+                    second.start()
 
     def arrive(name, side):
         slot, src, dst = plan[name, OPP[side]]
@@ -139,6 +201,14 @@
         @pl.when(has[side])
         def _():
             message(side, slot, src, dst).wait_recv()
+
+    def corner(which, side):
+        arrive(which, side)
+        left = core if which == "inner" else 1 - core
+        for direction, flag in ((LF, 1), (RT, 0)):
+            @pl.when(has[direction] & (left == flag))
+            def _():
+                message(direction, *plan["cor%d" % side, direction]).start()
 
     u, v = off_ref[0, 0, 0, 0], off_ref[0, 0, 0, 1]
     lane_row = lambda n: iota((n, B), 1)
@@ -194,14 +264,17 @@
 
     pl.semaphore_wait(
         barrier,
-        sum(h.astype(jnp.int32) for h in has),
+        sum(h.astype(jnp.int32) for h in has)
+        + 2 * is_relay.astype(jnp.int32)
+        + 4 * sum(c.astype(jnp.int32) for c in crossers),
     )
 
-    for name in ("off", "edge", "mid"):
+    for name in ("off", "outer", "inner", "mid"):
         go(name, UP)
         go(name, DN)
-    go("own", LF)
-    go("own", RT)
+    for name in ("own0", "own1"):
+        go(name, LF)
+        go(name, RT)
 
     loads[1].wait()
     for q in range(4):
@@ -232,6 +305,8 @@
     hi, lo = split(dot(hi, order_right) + dot(lo, order_right))
     meas[...] = jnp.sqrt((dot(order_left, hi) + dot(order_left, lo)) * PHOTON_SCALE)
 
+    corner("outer", UP)
+
     arrive("off", LF)
     arrive("off", RT)
     light[...] = jnp.zeros(light.shape, F32)
@@ -256,14 +331,14 @@
             light[r0:r0 + rn, c0:c0 + cn] += dot(hi, pick_col) + dot(lo, pick_col)
     light[...] = STEP_SIZE / (light[...] + REGULAR)
 
+    pass_on("own0", "own1")
+
     def put(rs, n, t, wr, wi):
         at = (slice(rs, rs + n), slice(POS[t] * B, (POS[t] + 1) * B))
         pr, pi = pp[(0,) + at], pp[(1,) + at]
         ex[(0,) + at] = pr * wr - pi * wi
         ex[(1,) + at] = pr * wi + pi * wr
 
-    arrive("own", LF)
-    arrive("own", RT)
     put(B, OWN, 1, obj[0, :, 0:B], obj[1, :, 0:B])
     put(B, OWN, 2, obj[0, :, B:256], obj[1, :, B:256])
 
@@ -273,16 +348,17 @@
         put(rs, n, 3, *(jnp.where(half, e, x) for e, x in zip(ends, back)))
         put(rs, n, 0, *(jnp.where(lane_row(n) < v, x, y_) for x, y_ in zip(back, from_left)))
 
+    loads[3].wait()
+    corner("outer", DN)
+    corner("inner", UP)
+    corner("inner", DN)
+    for name in ("own0", "own1"):
+        arrive(name, LF)
+        arrive(name, RT)
     side_tiles(
         B, OWN, [tail(0, OWN, ch) for ch in range(2)],
         [in_own[0, ch] for ch in range(2)], [in_own[1, ch] for ch in range(2)],
     )
-
-    loads[3].wait()
-    for side in (UP, DN):
-        arrive("edge", side)
-        go("cor%d" % side, LF)
-        go("cor%d" % side, RT)
     arrive("mid", UP)
     arrive("mid", DN)
 
@@ -405,7 +481,7 @@
             inner = lanes < v
             sg[0, c, m:m + n] = jnp.where(inner, 0.0, g0)
             sg[1, c, m:m + n] = roll64(jnp.where(lanes >= 64, g3, jnp.where(inner, g0, 0.0)))
-    for name in ("gcor", "gown"):
+    for name in ("gcor", "gown0", "gown1"):
         go(name, LF)
         go(name, RT)
     stage_left_out(1)
@@ -450,8 +526,11 @@
                     s_edge[side, e, c, h * 64:h * 64 + 64] = m[h] + o[h]
         go("gedge", side)
 
-    arrive("gown", LF)
-    arrive("gown", RT)
+    pass_on("gown0", "gown1")
+
+    for name in ("gown0", "gown1"):
+        arrive(name, LF)
+        arrive(name, RT)
     lanes = lane_row(OWN)
     for c in range(2):
         x = roll64(rg[1, c, 192:N])
@@ -477,9 +556,26 @@
             out_ref[c, at, 256:OWN] = last[:, 0:64]
 
     for (name, direction), (slot, src, dst) in plan.items():
-        @pl.when(has[direction])
+        if direction in (UP, DN) or name not in RELAYED:
+            @pl.when(has[direction])
+            def _():
+                message(direction, slot, src, dst).wait_send()
+            continue
+        crossing = col == CROSS[direction - LF]
+
+        @pl.when(has[direction] & jnp.logical_not(crossing))
         def _():
             message(direction, slot, src, dst).wait_send()
+
+        via, first, second = routed(name, direction)
+
+        @pl.when(crossing)
+        def _():
+            first.wait_send()
+
+        @pl.when(col == via)
+        def _():
+            second.wait_send()
 
 
 def local(rows, cols, object_slab, probe_field, offsets, counts):
@@ -503,6 +599,7 @@
             vmem((2, B, B), F32),
             vmem((2, 2, OWN, B), F32),
             vmem((2, 2, 2, B, B), F32),
+            vmem((2, 2, 160, B), F32),
             vmem((2, N, N), BF16),
             vmem((2, N, N), F32),
             vmem((N, N), F32),
@@ -523,8 +620,8 @@
             vmem((2, 2, 2, B, B), F32),
             vmem((2, B, B), F32),
             pltpu.SemaphoreType.DMA((4,)),
-            pltpu.SemaphoreType.DMA((22,)),
-            pltpu.SemaphoreType.DMA((22,)),
+            pltpu.SemaphoreType.DMA((30,)),
+            pltpu.SemaphoreType.DMA((30,)),
         ],
         compiler_params=pltpu.CompilerParams(
             collective_id=0, has_side_effects=True, vmem_limit_bytes=56 * 1024 * 1024

time: 57.6 us -> 54.6 us (0.948); the launches traced: 56.6 us -> 54.3 us
  Pallas kernels: 54.3 us -> 52 us
    pallas_call x1, Pallas kernels: 54.3 us -> 52 us  [local(): step(object_slab, probe_field, offsets, counts, jnp.asarray(tables()))]
where the time goes in v1:
time: 54.6 us; the launch traced here: 54.3 us
  Pallas kernels  52 us (95%)
  other arithmetic  2.25 us (4%)
    pallas_call x1, Pallas kernels, local(): step(object_slab, probe_field, offsets, counts, jnp.asarray(tables()))  52 us
    sub x1, other arithmetic, local(): object_slab - step(object_slab, probe_field, offsets, counts, jnp.asarray...  2.25 us

profile of v1, /device:TPU:161, one launch (start us, length us, event | category | flops | bytes accessed | tf_op | source)
XLA Modules:
  0.0 54.3 jit_solution(3465771088377841396)
XLA Ops:
  0.0 0.0 copy-start
  0.0 52.0 %step.1 = f32[2,320,320]{2,1,0:T(8,128)} custom-call(f32[2,320,320]{2,1,0:T(8,128)} %obj_hbm.1, f32[2,512,512]{2,1,0:T(8,128)} %probe_hbm.1, s32[1,1,1,2]{3,2,1,0:T(1,128)} %off_ref.1, s32[1,1,1,512,512]{4,3,2,1,0:T(8,128)} %counts_hbm.1, bf16[2,2,4,256,256]{4,3,2,1,0:T(8,128)(2,1)} %constant.2.clone.tab_hbm), custom_call_target="tpu_custom_call" | custom-call | tf_op jit(solution)/shard_map/step/pallas_call | solution.py:631
  52.0 0.0 copy-done
  52.0 2.2 %sub.3 = f32[2,320,320]{2,1,0:T(8,128)} subtract(f32[2,320,320]{2,1,0:T(8,128)S(1)} %copy-done, f32[2,320,320]{2,1,0:T(8,128)} %step.1) | non-fusion elementwise | flops 204800 | bytes 2457600 | tf_op jit(solution)/shard_map/sub | solution.py:631
Async XLA Ops:
  0.0 52.0 %copy-start = (f32[2,320,320]{2,1,0:T(8,128)S(1)}, f32[2,320,320]{2,1,0:T(8,128)}, u32[]{:S(2)}) copy-start(f32[2,320,320]{2,1,0:T(8,128)} %obj_hbm.1) | copy-start | bytes 2457604

commit v2 on v1

--- a/solution.py
+++ b/solution.py
@@ -65,7 +65,7 @@
     out_ref,
     obj, probe, counts, tab, offs, edge, mid_up, mid_dn,
     in_edge, in_mid, in_own, in_cor, relay_in,
-    lum, pp, meas, light, ex, zh, zl, y, kh, kl, w, acc, g, sg, rg, s_edge, s_mid, r_edge, r_mid,
+    lum, pp, meas, light, ex, zh, zl, y, back, kh, kl, w, acc, g, sg, rg, s_edge, s_mid, r_edge, r_mid,
     load_sem, send_sem, recv_sem,
 ):
     row, col = lax.axis_index("row"), lax.axis_index("col")
@@ -95,8 +95,11 @@
 
     OPP = (DN, UP, RT, LF)
     CROSS = (8, 7)
-    RELAYS = {LF: (5, 3), RT: (11, 13)}
-    RELAYED = ("own0", "own1", "gown0", "gown1")
+    RELAYS = {LF: (5, 3, 1), RT: (11, 13, 15)}
+    OWNS, GOWN = ("own0", "own1", "own2"), ("gown0", "gown1", "gown2")
+    RELAYED = OWNS + GOWN
+    PARTS = (slice(0, 104), slice(104, 208), slice(208, OWN))
+    GPARTS = tuple(slice(192 + p.start, 192 + p.stop) for p in PARTS)
     crossers = [(col == c) for c in CROSS]
     is_relay = functools.reduce(
         jnp.logical_or, [col == c for d in (LF, RT) for c in RELAYS[d]]
@@ -134,32 +137,28 @@
         ("mid", DN): (5, mid_dn, in_mid.at[0]),
         ("off", LF): (6, offs.at[1], offs.at[2]),
         ("off", RT): (7, offs.at[1], offs.at[0]),
-        ("own0", LF): (8, edge.at[0, :, 0:160], in_own.at[1, :, 0:160]),
-        ("own0", RT): (9, edge.at[1, :, 0:160], in_own.at[0, :, 0:160]),
-        ("own1", LF): (22, edge.at[0, :, 160:OWN], in_own.at[1, :, 160:OWN]),
-        ("own1", RT): (23, edge.at[1, :, 160:OWN], in_own.at[0, :, 160:OWN]),
-        ("cor0", LF): (10, in_edge.at[0, 0], in_cor.at[1, 0]),
-        ("cor0", RT): (11, in_edge.at[0, 1], in_cor.at[0, 0]),
-        ("cor1", LF): (12, in_edge.at[1, 0], in_cor.at[1, 1]),
-        ("cor1", RT): (13, in_edge.at[1, 1], in_cor.at[0, 1]),
-        ("gcor", LF): (14, sg.at[0, :, 0:192], rg.at[1, :, 0:192]),
-        ("gcor", RT): (15, sg.at[1, :, 0:192], rg.at[0, :, 0:192]),
-        ("gown0", LF): (16, sg.at[0, :, 192:352], rg.at[1, :, 192:352]),
-        ("gown0", RT): (17, sg.at[1, :, 192:352], rg.at[0, :, 192:352]),
-        ("gown1", LF): (24, sg.at[0, :, 352:N], rg.at[1, :, 352:N]),
-        ("gown1", RT): (25, sg.at[1, :, 352:N], rg.at[0, :, 352:N]),
+        **{(OWNS[k], LF): (8 + 2 * k, edge.at[0, :, p], in_own.at[1, :, p]) for k, p in enumerate(PARTS)},
+        **{(OWNS[k], RT): (9 + 2 * k, edge.at[1, :, p], in_own.at[0, :, p]) for k, p in enumerate(PARTS)},
+        ("cor0", LF): (16, in_edge.at[0, 0], in_cor.at[1, 0]),
+        ("cor0", RT): (17, in_edge.at[0, 1], in_cor.at[0, 0]),
+        ("cor1", LF): (22, in_edge.at[1, 0], in_cor.at[1, 1]),
+        ("cor1", RT): (23, in_edge.at[1, 1], in_cor.at[0, 1]),
+        ("gcor", LF): (24, sg.at[0, :, 0:192], rg.at[1, :, 0:192]),
+        ("gcor", RT): (25, sg.at[1, :, 0:192], rg.at[0, :, 0:192]),
+        **{(GOWN[k], LF): (34 + 2 * k, sg.at[0, :, p], rg.at[1, :, p]) for k, p in enumerate(GPARTS)},
+        **{(GOWN[k], RT): (35 + 2 * k, sg.at[1, :, p], rg.at[0, :, p]) for k, p in enumerate(GPARTS)},
         ("gmid", UP): (18, s_mid.at[0], r_mid.at[1]),
         ("gmid", DN): (19, s_mid.at[1], r_mid.at[0]),
-        ("gedge", UP): (20, s_edge.at[0], r_edge.at[1]),
-        ("gedge", DN): (21, s_edge.at[1], r_edge.at[0]),
+        ("gedge0", UP): (20, s_edge.at[0, 0], r_edge.at[1, 0]),
+        ("gedge0", DN): (21, s_edge.at[1, 0], r_edge.at[0, 0]),
+        ("gedge1", UP): (30, s_edge.at[0, 1], r_edge.at[1, 1]),
+        ("gedge1", DN): (31, s_edge.at[1, 1], r_edge.at[0, 1]),
     }
 
     def routed(name, direction):
         slot, src, dst = plan[name, direction]
-        k, held, held_slot = {
-            "own0": (0, relay_in.at[0], 26), "own1": (1, relay_in.at[0], 26),
-            "gown0": (0, relay_in.at[1], 27), "gown1": (1, relay_in.at[1], 27),
-        }[name]
+        k, phase = int(name[-1]), 0 if name in OWNS else 1
+        held, held_slot = relay_in.at[phase, :, 0:PARTS[k].stop - PARTS[k].start], 26 + phase
 
         def leg(source, target, sent, received, to):
             return pltpu.make_async_remote_copy(
@@ -169,7 +168,11 @@
             )
 
         via, end = RELAYS[direction][k], CROSS[1 - (direction - LF)]
-        return via, leg(src, held, slot, held_slot, via), leg(held, dst, held_slot, slot, end)
+        return (
+            via,
+            lambda: leg(src, held, slot, held_slot, via),
+            lambda: leg(held, dst, held_slot, slot, end),
+        )
 
     def go(name, direction):
         if direction not in (LF, RT) or name not in RELAYED:
@@ -183,7 +186,7 @@
 
         @pl.when(crossing)
         def _():
-            routed(name, direction)[1].start()
+            routed(name, direction)[1]().start()
 
     def pass_on(*names):
         for name in names:
@@ -192,8 +195,8 @@
 
                 @pl.when(col == via)
                 def _():
-                    first.wait_recv()
-                    second.start()
+                    first().wait_recv()
+                    second().start()
 
     def arrive(name, side):
         slot, src, dst = plan[name, OPP[side]]
@@ -266,13 +269,13 @@
         barrier,
         sum(h.astype(jnp.int32) for h in has)
         + 2 * is_relay.astype(jnp.int32)
-        + 4 * sum(c.astype(jnp.int32) for c in crossers),
+        + 6 * sum(c.astype(jnp.int32) for c in crossers),
     )
 
     for name in ("off", "outer", "inner", "mid"):
         go(name, UP)
         go(name, DN)
-    for name in ("own0", "own1"):
+    for name in OWNS:
         go(name, LF)
         go(name, RT)
 
@@ -285,7 +288,7 @@
         lum[1, rs] = lo
     d = iota((N, N), 0) + v - ((iota((N, N), 1) + 3 * B) % N)
     right = onehot((d == 0) | (d == N))
-    d = iota((N, N), 1) + u - iota((N, N), 0)
+    d = iota((N, N), 1) + u - (iota((N, N), 0) + 448) % N
     left = onehot((d == 0) | (d == N))
     for ch in range(2):
         hi, lo = split(probe[ch])
@@ -331,57 +334,7 @@
             light[r0:r0 + rn, c0:c0 + cn] += dot(hi, pick_col) + dot(lo, pick_col)
     light[...] = STEP_SIZE / (light[...] + REGULAR)
 
-    pass_on("own0", "own1")
-
-    def put(rs, n, t, wr, wi):
-        at = (slice(rs, rs + n), slice(POS[t] * B, (POS[t] + 1) * B))
-        pr, pi = pp[(0,) + at], pp[(1,) + at]
-        ex[(0,) + at] = pr * wr - pi * wi
-        ex[(1,) + at] = pr * wi + pi * wr
-
-    put(B, OWN, 1, obj[0, :, 0:B], obj[1, :, 0:B])
-    put(B, OWN, 2, obj[0, :, B:256], obj[1, :, B:256])
-
-    def side_tiles(rs, n, ends, from_left, from_right):
-        half = lane_row(n) < 64
-        back = [roll64(x) for x in from_right]
-        put(rs, n, 3, *(jnp.where(half, e, x) for e, x in zip(ends, back)))
-        put(rs, n, 0, *(jnp.where(lane_row(n) < v, x, y_) for x, y_ in zip(back, from_left)))
-
-    loads[3].wait()
-    corner("outer", DN)
-    corner("inner", UP)
-    corner("inner", DN)
-    for name in ("own0", "own1"):
-        arrive(name, LF)
-        arrive(name, RT)
-    side_tiles(
-        B, OWN, [tail(0, OWN, ch) for ch in range(2)],
-        [in_own[0, ch] for ch in range(2)], [in_own[1, ch] for ch in range(2)],
-    )
-    arrive("mid", UP)
-    arrive("mid", DN)
-
-    groups = (0, 64, 448)
-    row64 = iota((64, B), 0)
-
-    def halo(group, get):
-        if group == 0:
-            return jnp.where(row64 < u, get(1, 64), get(0, 0))
-        if group == 64:
-            return get(0, 64)
-        return get(1, 0)
-
-    def rolled_edge(group, ch):
-        return roll64(halo(group, lambda s, r: in_edge[s, 1, ch, r:r + 64]))
-
-    for rs in groups:
-        put(rs, 64, 1, *(halo(rs, lambda s, r: in_edge[s, 0, ch, r:r + 64]) for ch in range(2)))
-        m = halo(rs, lambda s, r: in_mid[s, r:r + 64])
-        put(rs, 64, 2, *(
-            jnp.where(low_half, m if ch == 0 else roll64(m), rolled_edge(rs, ch))
-            for ch in range(2)
-        ))
+    pass_on(*OWNS)
 
     def fwd4(x):
         (ar, ai), (br, bi), (cr, ci), (dr_, di) = x
@@ -401,22 +354,88 @@
             (er - gr, ei - gi), (fr + hi_, fi - hr),
         ]
 
-    def stage_left_in(p):
-        ls = slice(p * 256, p * 256 + 256)
-        z = fwd4([(ex[0, q * B:(q + 1) * B, ls], ex[1, q * B:(q + 1) * B, ls]) for q in range(4)])
-        for r in range(4):
+    def dot3(a_hi, a_lo, b_hi, b_lo):
+        return dot(a_hi, b_hi) + dot(a_hi, b_lo) + dot(a_lo, b_hi)
+
+    def columns_in(rs):
+        z = fwd4([
+            tuple(ex[c, rs, POS[q] * B:(POS[q] + 1) * B] for c in range(2)) for q in range(4)
+        ])
+        for f in range(4):
             for c in range(2):
-                hi, lo = split(z[r][c])
-                zh[r, c * B:(c + 1) * B, ls] = hi
-                zl[r, c * B:(c + 1) * B, ls] = lo
-        for r in range(4):
-            y[r, :, ls] = (
-                dot(tab[0, 0, r], zh[r, :, ls])
-                + dot(tab[0, 0, r], zl[r, :, ls])
-                + dot(tab[1, 0, r], zh[r, :, ls])
-            )
-
-    stage_left_in(1)
+                hi, lo = split(z[f][c])
+                kh[f, rs, c * B:(c + 1) * B] = hi
+                kl[f, rs, c * B:(c + 1) * B] = lo
+        for f in range(4):
+            out = dot3(kh[f, rs], kl[f, rs], tab[0, 1, f], tab[1, 1, f])
+            for c in range(2):
+                y[c, rs, f * B:(f + 1) * B] = out[:, c * B:(c + 1) * B]
+
+    def columns_out(rs):
+        for f in range(4):
+            w[f, rs] = dot3(kh[f, rs], kl[f, rs], tab[0, 0, f], tab[1, 0, f])
+        x = inv4([(w[f, rs, 0:B], w[f, rs, B:256]) for f in range(4)])
+        for q in range(4):
+            ls = slice(POS[q] * B, (POS[q] + 1) * B)
+            pr, pi = pp[0, rs, ls], pp[1, rs, ls]
+            br, bi = x[q]
+            g[0, rs, ls] = pr * br + pi * bi
+            g[1, rs, ls] = pr * bi - pi * br
+
+    MARGIN, INSIDE = slice(0, 192), slice(192, N)
+
+    def put(rs, n, t, wr, wi):
+        m = (rs + 64) % N
+        at = (slice(m, m + n), slice(POS[t] * B, (POS[t] + 1) * B))
+        pr, pi = pp[(0,) + at], pp[(1,) + at]
+        ex[(0,) + at] = pr * wr - pi * wi
+        ex[(1,) + at] = pr * wi + pi * wr
+
+    put(B, OWN, 1, obj[0, :, 0:B], obj[1, :, 0:B])
+    put(B, OWN, 2, obj[0, :, B:256], obj[1, :, B:256])
+
+    def side_tiles(rs, n, ends, from_left, from_right):
+        half = lane_row(n) < 64
+        back = [roll64(x) for x in from_right]
+        put(rs, n, 3, *(jnp.where(half, e, x) for e, x in zip(ends, back)))
+        put(rs, n, 0, *(jnp.where(lane_row(n) < v, x, y_) for x, y_ in zip(back, from_left)))
+
+    loads[3].wait()
+    corner("outer", DN)
+    corner("inner", UP)
+    corner("inner", DN)
+    for name in OWNS:
+        arrive(name, LF)
+        arrive(name, RT)
+    side_tiles(
+        B, OWN, [tail(0, OWN, ch) for ch in range(2)],
+        [in_own[0, ch] for ch in range(2)], [in_own[1, ch] for ch in range(2)],
+    )
+    columns_in(INSIDE)
+    arrive("mid", UP)
+    arrive("mid", DN)
+
+    groups = (0, 64, 448)
+    row64 = iota((64, B), 0)
+
+    def halo(group, get):
+        if group == 0:
+            return jnp.where(row64 < u, get(1, 64), get(0, 0))
+        if group == 64:
+            return get(0, 64)
+        return get(1, 0)
+
+    def rolled_edge(group, ch):
+        return roll64(halo(group, lambda s, r: in_edge[s, 1, ch, r:r + 64]))
+
+    for rs in groups:
+        put(rs, 64, 1, *(halo(rs, lambda s, r: in_edge[s, 0, ch, r:r + 64]) for ch in range(2)))
+        m = halo(rs, lambda s, r: in_mid[s, r:r + 64])
+        put(rs, 64, 2, *(
+            jnp.where(low_half, m if ch == 0 else roll64(m), rolled_edge(rs, ch))
+            for ch in range(2)
+        ))
+
     for side in (UP, DN):
         arrive("cor%d" % side, LF)
         arrive("cor%d" % side, RT)
@@ -426,65 +445,51 @@
             [halo(rs, lambda s, r: in_cor[0, s, ch, r:r + 64]) for ch in range(2)],
             [halo(rs, lambda s, r: in_cor[1, s, ch, r:r + 64]) for ch in range(2)],
         )
-    stage_left_in(0)
-
-    def dot3(a_hi, a_lo, b_hi, b_lo):
-        return dot(a_hi, b_hi) + dot(a_hi, b_lo) + dot(a_lo, b_hi)
-
+    columns_in(MARGIN)
+
+    def block(ref, c, q):
+        if q < 3:
+            return ref[c, 64 + q * B:64 + (q + 1) * B]
+        return jnp.concatenate([ref[c, 448:N], ref[c, 0:64]], axis=0)
+
+    z = fwd4([tuple(block(y, c, q) for c in range(2)) for q in range(4)])
     for r in range(4):
-        z = fwd4([
-            tuple(y[r, c * B:(c + 1) * B, POS[q] * B:(POS[q] + 1) * B] for c in range(2))
-            for q in range(4)
-        ])
-        for s in range(4):
-            for c in range(2):
-                hi, lo = split(z[s][c])
-                kh[s, r * B:(r + 1) * B, c * B:(c + 1) * B] = hi
-                kl[s, r * B:(r + 1) * B, c * B:(c + 1) * B] = lo
-    for s in range(4):
-        far = dot3(kh[s], kl[s], tab[0, 1, s], tab[1, 1, s])
-        fr, fi = far[:, 0:B], far[:, B:256]
-        factor = 1.0 - meas[:, s * B:(s + 1) * B] * lax.rsqrt(fr * fr + fi * fi + EPSILON)
-        hi, lo = split(jnp.concatenate([factor * fr, factor * fi], axis=1))
-        w[s] = dot3(hi, lo, tab[0, 0, s], tab[1, 0, s])
-
+        for c in range(2):
+            hi, lo = split(z[r][c])
+            zh[r, c * B:(c + 1) * B] = hi
+            zl[r, c * B:(c + 1) * B] = lo
     for r in range(4):
-        rs = slice(r * B, (r + 1) * B)
-        x = inv4([(w[s, rs, 0:B], w[s, rs, B:256]) for s in range(4)])
-        for q in range(4):
-            for c in range(2):
-                hi, lo = split(x[q][c])
-                zh[r, c * B:(c + 1) * B, POS[q] * B:(POS[q] + 1) * B] = hi
-                zl[r, c * B:(c + 1) * B, POS[q] * B:(POS[q] + 1) * B] = lo
-
-    def stage_left_out(p):
-        ls = slice(p * 256, p * 256 + 256)
-        for r in range(4):
-            y[r, :, ls] = (
-                dot(tab[0, 1, r], zh[r, :, ls])
-                + dot(tab[0, 1, r], zl[r, :, ls])
-                + dot(tab[1, 1, r], zh[r, :, ls])
-            )
-        x = inv4([(y[r, 0:B, ls], y[r, B:256, ls]) for r in range(4)])
-        for q in range(4):
-            rs = slice(q * B, (q + 1) * B)
-            pr, pi = pp[0, rs, ls], pp[1, rs, ls]
-            br, bi = x[q]
-            g[0, rs, ls] = pr * br + pi * bi
-            g[1, rs, ls] = pr * bi - pi * br
-
-    stage_left_out(0)
-    for rs, n, m in ((448, 64, 0), (0, 448, 64)):
-        lanes = lane_row(n)
+        far = dot3(tab[0, 0, r], tab[1, 0, r], zh[r], zl[r])
+        fr, fi = far[0:B], far[B:256]
+        factor = 1.0 - meas[r * B:(r + 1) * B] * lax.rsqrt(fr * fr + fi * fi + EPSILON)
+        hi, lo = split(jnp.concatenate([factor * fr, factor * fi], axis=0))
+        back[r] = dot3(tab[0, 1, r], tab[1, 1, r], hi, lo)
+    x = inv4([(back[r, 0:B], back[r, B:256]) for r in range(4)])
+    for q in range(4):
         for c in range(2):
-            g3, g0 = g[c, rs:rs + n, 0:B], g[c, rs:rs + n, B:256]
-            inner = lanes < v
-            sg[0, c, m:m + n] = jnp.where(inner, 0.0, g0)
-            sg[1, c, m:m + n] = roll64(jnp.where(lanes >= 64, g3, jnp.where(inner, g0, 0.0)))
-    for name in ("gcor", "gown0", "gown1"):
-        go(name, LF)
-        go(name, RT)
-    stage_left_out(1)
+            parts = split(x[q][c])
+            for f in range(4):
+                for ref, part in zip((kh, kl), parts):
+                    piece = part[:, f * B:(f + 1) * B]
+                    at = slice(c * B, (c + 1) * B)
+                    if q < 3:
+                        ref[f, 64 + q * B:64 + (q + 1) * B, at] = piece
+                    else:
+                        ref[f, 448:N, at] = piece[0:64]
+                        ref[f, 0:64, at] = piece[64:B]
+
+    def to_sides(rs):
+        lanes = lane_row(rs.stop - rs.start)
+        inner = lanes < v
+        for c in range(2):
+            g3, g0 = g[c, rs, 0:B], g[c, rs, B:256]
+            sg[0, c, rs] = jnp.where(inner, 0.0, g0)
+            sg[1, c, rs] = roll64(jnp.where(lanes >= 64, g3, jnp.where(inner, g0, 0.0)))
+
+    columns_out(MARGIN)
+    to_sides(MARGIN)
+    go("gcor", LF)
+    go("gcor", RT)
 
     row64f = row64.astype(F32)
 
@@ -496,7 +501,8 @@
     own_u = offs[1, 1, 0:1, :]
 
     def tile(c, rs, n, t):
-        return g[c, rs:rs + n, POS[t] * B:(POS[t] + 1) * B]
+        m = (rs + 64) % N
+        return g[c, m:m + n, POS[t] * B:(POS[t] + 1) * B]
 
     for side in (UP, DN):
         m = outgoing(
@@ -507,16 +513,24 @@
         for h in range(2):
             s_mid[side, h * 64:h * 64 + 64] = m[h]
         go("gmid", side)
-    arrive("gcor", LF)
-    arrive("gcor", RT)
-    for side in (UP, DN):
-        for c in range(2):
-            mine = (
-                lambda rs: tile(c, rs, 64, 1),
-                lambda rs: roll64(jnp.where(low_half, tile(c, rs, 64, 3), tile(c, rs, 64, 2))),
-            )
-            for e in range(2):
-                m = outgoing(side, mine[e], own_u)
+
+    columns_out(INSIDE)
+    to_sides(INSIDE)
+    for name in GOWN:
+        go(name, LF)
+        go(name, RT)
+
+    def edges(e):
+        arrive("gcor", LF if e == 0 else RT)
+        for side in (UP, DN):
+            for c in range(2):
+                if e == 0:
+                    mine = lambda rs: tile(c, rs, 64, 1)
+                else:
+                    mine = lambda rs: roll64(
+                        jnp.where(low_half, tile(c, rs, 64, 3), tile(c, rs, 64, 2))
+                    )
+                m = outgoing(side, mine, own_u)
                 o = outgoing(
                     side,
                     lambda rs: rg[e, c, (rs + 64) % N:(rs + 64) % N + 64],
@@ -524,11 +538,17 @@
                 )
                 for h in range(2):
                     s_edge[side, e, c, h * 64:h * 64 + 64] = m[h] + o[h]
-        go("gedge", side)
-
-    pass_on("gown0", "gown1")
-
-    for name in ("gown0", "gown1"):
+            go("gedge%d" % e, side)
+
+    for which in ("ginner", "gouter"):
+        for e in range(2):
+            @pl.when(core == (1 - e if which == "ginner" else e))
+            def _():
+                edges(e)
+
+    pass_on(*GOWN)
+
+    for name in GOWN:
         arrive(name, LF)
         arrive(name, RT)
     lanes = lane_row(OWN)
@@ -543,7 +563,8 @@
 
     for side, rs in ((UP, 0), (DN, 192)):
         arrive("gmid", side)
-        arrive("gedge", side)
+        arrive("gedge0", side)
+        arrive("gedge1", side)
         at = slice(rs, rs + B)
         for c in range(2):
             x = roll64(r_edge[side, 1, c])
@@ -571,11 +592,11 @@
 
         @pl.when(crossing)
         def _():
-            first.wait_send()
+            first().wait_send()
 
         @pl.when(col == via)
         def _():
-            second.wait_send()
+            second().wait_send()
 
 
 def local(rows, cols, object_slab, probe_field, offsets, counts):
@@ -583,7 +604,7 @@
     vmem = pltpu.VMEM
     step = pl.pallas_call(
         functools.partial(kernel, rows, cols),
-        out_shape=jax.ShapeDtypeStruct((2, OWN, OWN), F32),
+        out_shape=pltpu.VMEM((2, OWN, OWN), F32),
         in_specs=[hbm, hbm, pl.BlockSpec(memory_space=pltpu.SMEM), hbm, hbm],
         out_specs=pl.BlockSpec(memory_space=pltpu.VMEM),
         scratch_shapes=[
@@ -599,7 +620,7 @@
             vmem((2, B, B), F32),
             vmem((2, 2, OWN, B), F32),
             vmem((2, 2, 2, B, B), F32),
-            vmem((2, 2, 160, B), F32),
+            vmem((2, 2, 112, B), F32),
             vmem((2, N, N), BF16),
             vmem((2, N, N), F32),
             vmem((N, N), F32),
@@ -607,6 +628,7 @@
             vmem((2, N, N), F32),
             vmem((4, 256, N), BF16),
             vmem((4, 256, N), BF16),
+            vmem((2, N, N), F32),
             vmem((4, 256, N), F32),
             vmem((4, N, 256), BF16),
             vmem((4, N, 256), BF16),
@@ -620,8 +642,8 @@
             vmem((2, 2, 2, B, B), F32),
             vmem((2, B, B), F32),
             pltpu.SemaphoreType.DMA((4,)),
-            pltpu.SemaphoreType.DMA((30,)),
-            pltpu.SemaphoreType.DMA((30,)),
+            pltpu.SemaphoreType.DMA((40,)),
+            pltpu.SemaphoreType.DMA((40,)),
         ],
         compiler_params=pltpu.CompilerParams(
             collective_id=0, has_side_effects=True, vmem_limit_bytes=56 * 1024 * 1024

time: 54.6 us -> 50.2 us (0.919)
  Pallas kernels: 52 us -> 49.1 us
  other arithmetic: 2.25 us -> 1.04 us
    pallas_call x1, Pallas kernels: 52 us -> 49.1 us  [local(): step(object_slab, probe_field, offsets, counts, jnp.asarray(tables()))]
    sub x1, other arithmetic: 2.25 us -> 1.04 us  [local(): object_slab - step(object_slab, probe_field, offsets, counts, jnp.asarray...]
where the time goes in v2:
time: 50.2 us; the launch traced here: 50.1 us
  Pallas kernels  49.1 us (98%)
  other arithmetic  1.04 us (2%)
    pallas_call x1, Pallas kernels, local(): step(object_slab, probe_field, offsets, counts, jnp.asarray(tables()))  49.1 us
    sub x1, other arithmetic, local(): object_slab - step(object_slab, probe_field, offsets, counts, jnp.asarray...  1.04 us

profile of v2, /device:TPU:161, one launch (start us, length us, event | category | flops | bytes accessed | tf_op | source)
XLA Modules:
  0.0 50.1 jit_solution(4896175630751788656)
XLA Ops:
  0.0 0.0 copy-start
  0.0 49.1 %step.1 = f32[2,320,320]{2,1,0:T(8,128)S(1)} custom-call(f32[2,320,320]{2,1,0:T(8,128)} %obj_hbm.1, f32[2,512,512]{2,1,0:T(8,128)} %probe_hbm.1, s32[1,1,1,2]{3,2,1,0:T(1,128)} %off_ref.1, s32[1,1,1,512,512]{4,3,2,1,0:T(8,128)} %counts_hbm.1, bf16[2,2,4,256,256]{4,3,2,1,0:T(8,128)(2,1)} %constant.2.clone.tab_hbm), custom_call_target="tpu_custom_call" | custom-call | tf_op jit(solution)/shard_map/step/pallas_call | solution.py:653
  49.1 0.0 copy-done
  49.1 1.0 %sub.3 = f32[2,320,320]{2,1,0:T(8,128)} subtract(f32[2,320,320]{2,1,0:T(8,128)S(1)} %copy-done, f32[2,320,320]{2,1,0:T(8,128)S(1)} %step.1) | non-fusion elementwise | flops 204800 | bytes 2457600 | tf_op jit(solution)/shard_map/sub | solution.py:653
Async XLA Ops:
  0.0 49.1 %copy-start = (f32[2,320,320]{2,1,0:T(8,128)S(1)}, f32[2,320,320]{2,1,0:T(8,128)}, u32[]{:S(2)}) copy-start(f32[2,320,320]{2,1,0:T(8,128)} %obj_hbm.1) | copy-start | bytes 2457604

commit v3 on v2

--- a/solution.py
+++ b/solution.py
@@ -61,9 +61,9 @@
 
 def kernel(
     rows, cols,
-    obj_hbm, probe_hbm, off_ref, counts_hbm, tab_hbm,
+    obj_hbm, probe_hbm, off_hbm, counts_hbm, tab_hbm,
     out_ref,
-    obj, probe, counts, tab, offs, edge, mid_up, mid_dn,
+    off_ref, obj, probe, counts, tab, offs, edge, mid_up, mid_dn,
     in_edge, in_mid, in_own, in_cor, relay_in,
     lum, pp, meas, light, ex, zh, zl, y, back, kh, kl, w, acc, g, sg, rg, s_edge, s_mid, r_edge, r_mid,
     load_sem, send_sem, recv_sem,
@@ -83,6 +83,7 @@
         load(probe_hbm, probe, 1),
         load(counts_hbm.at[0, 0, 0], counts, 2),
         load(tab_hbm, tab, 3),
+        load(off_hbm, off_ref, 4),
     ]
     for c in loads:
         c.start()
@@ -96,10 +97,10 @@
     OPP = (DN, UP, RT, LF)
     CROSS = (8, 7)
     RELAYS = {LF: (5, 3, 1), RT: (11, 13, 15)}
-    OWNS, GOWN = ("own0", "own1", "own2"), ("gown0", "gown1", "gown2")
-    RELAYED = OWNS + GOWN
-    PARTS = (slice(0, 104), slice(104, 208), slice(208, OWN))
-    GPARTS = tuple(slice(192 + p.start, 192 + p.stop) for p in PARTS)
+    OWNS, GOWN = ("own0", "own1"), ("gown0", "gown1", "gown2")
+    RELAYED = OWNS + ("cor0",) + GOWN
+    PARTS = (slice(0, 160), slice(160, OWN))
+    GPARTS = (slice(192, 296), slice(296, 400), slice(400, N))
     crossers = [(col == c) for c in CROSS]
     is_relay = functools.reduce(
         jnp.logical_or, [col == c for d in (LF, RT) for c in RELAYS[d]]
@@ -157,8 +158,8 @@
 
     def routed(name, direction):
         slot, src, dst = plan[name, direction]
-        k, phase = int(name[-1]), 0 if name in OWNS else 1
-        held, held_slot = relay_in.at[phase, :, 0:PARTS[k].stop - PARTS[k].start], 26 + phase
+        k, phase = 2 if name == "cor0" else int(name[-1]), 0 if name[0] != "g" else 1
+        held, held_slot = relay_in.at[phase, :, 0:src.shape[-2]], 26 + phase
 
         def leg(source, target, sent, received, to):
             return pltpu.make_async_remote_copy(
@@ -188,6 +189,11 @@
         def _():
             routed(name, direction)[1]().start()
 
+    def gone(name, direction):
+        @pl.when(has[direction])
+        def _():
+            message(direction, *plan[name, direction]).wait_send()
+
     def pass_on(*names):
         for name in names:
             for direction in (LF, RT):
@@ -209,11 +215,10 @@
         arrive(which, side)
         left = core if which == "inner" else 1 - core
         for direction, flag in ((LF, 1), (RT, 0)):
-            @pl.when(has[direction] & (left == flag))
+            @pl.when(left == flag)
             def _():
-                message(direction, *plan["cor%d" % side, direction]).start()
-
-    u, v = off_ref[0, 0, 0, 0], off_ref[0, 0, 0, 1]
+                go("cor%d" % side, direction)
+
     lane_row = lambda n: iota((n, B), 1)
     low_half = lane_row(64) < 64
 
@@ -247,6 +252,8 @@
         rg[1] = jnp.zeros(rg.shape[1:], F32)
         offs[2] = jnp.full((3, 8, B), NOWHERE, F32)
 
+    loads[4].wait()
+    u, v = off_ref[0, 0, 0, 0], off_ref[0, 0, 0, 1]
     uf, vf = u.astype(F32), v.astype(F32)
     offs[1, 1] = jnp.where(iota((8, B), 0) == 0, uf, vf)
 
@@ -272,7 +279,7 @@
         + 6 * sum(c.astype(jnp.int32) for c in crossers),
     )
 
-    for name in ("off", "outer", "inner", "mid"):
+    for name in ("off", "outer"):
         go(name, UP)
         go(name, DN)
     for name in OWNS:
@@ -308,6 +315,10 @@
     hi, lo = split(dot(hi, order_right) + dot(lo, order_right))
     meas[...] = jnp.sqrt((dot(order_left, hi) + dot(order_left, lo)) * PHOTON_SCALE)
 
+    for direction in (UP, DN):
+        gone("outer", direction)
+    go("inner", UP)
+    go("inner", DN)
     corner("outer", UP)
 
     arrive("off", LF)
@@ -402,6 +413,11 @@
 
     loads[3].wait()
     corner("outer", DN)
+    pass_on("cor0")
+    for direction in (UP, DN):
+        gone("inner", direction)
+    go("mid", UP)
+    go("mid", DN)
     corner("inner", UP)
     corner("inner", DN)
     for name in OWNS:
@@ -487,9 +503,6 @@
             sg[1, c, rs] = roll64(jnp.where(lanes >= 64, g3, jnp.where(inner, g0, 0.0)))
 
     columns_out(MARGIN)
-    to_sides(MARGIN)
-    go("gcor", LF)
-    go("gcor", RT)
 
     row64f = row64.astype(F32)
 
@@ -513,6 +526,9 @@
         for h in range(2):
             s_mid[side, h * 64:h * 64 + 64] = m[h]
         go("gmid", side)
+    to_sides(MARGIN)
+    go("gcor", LF)
+    go("gcor", RT)
 
     columns_out(INSIDE)
     to_sides(INSIDE)
@@ -577,6 +593,8 @@
             out_ref[c, at, 256:OWN] = last[:, 0:64]
 
     for (name, direction), (slot, src, dst) in plan.items():
+        if name in ("outer", "inner"):
+            continue
         if direction in (UP, DN) or name not in RELAYED:
             @pl.when(has[direction])
             def _():
@@ -605,9 +623,10 @@
     step = pl.pallas_call(
         functools.partial(kernel, rows, cols),
         out_shape=pltpu.VMEM((2, OWN, OWN), F32),
-        in_specs=[hbm, hbm, pl.BlockSpec(memory_space=pltpu.SMEM), hbm, hbm],
+        in_specs=[hbm] * 5,
         out_specs=pl.BlockSpec(memory_space=pltpu.VMEM),
         scratch_shapes=[
+            pltpu.SMEM((1, 1, 1, 2), jnp.int32),
             vmem((2, OWN, OWN), F32),
             vmem((2, N, N), F32),
             vmem((N, N), jnp.int32),
@@ -620,7 +639,7 @@
             vmem((2, B, B), F32),
             vmem((2, 2, OWN, B), F32),
             vmem((2, 2, 2, B, B), F32),
-            vmem((2, 2, 112, B), F32),
+            vmem((2, 2, 160, B), F32),
             vmem((2, N, N), BF16),
             vmem((2, N, N), F32),
             vmem((N, N), F32),
@@ -641,7 +660,7 @@
             vmem((2, B, B), F32),
             vmem((2, 2, 2, B, B), F32),
             vmem((2, B, B), F32),
-            pltpu.SemaphoreType.DMA((4,)),
+            pltpu.SemaphoreType.DMA((5,)),
             pltpu.SemaphoreType.DMA((40,)),
             pltpu.SemaphoreType.DMA((40,)),
         ],

time: 50.2 us -> 47.7 us (0.950); the launches traced: 50.1 us -> 46.9 us
  Pallas kernels: 49.1 us -> 45.9 us
    pallas_call x1, Pallas kernels: 49.1 us -> 45.9 us  [local(): step(object_slab, probe_field, offsets, counts, jnp.asarray(tables()))]
where the time goes in v3:
time: 47.7 us; the launch traced here: 46.9 us
  Pallas kernels  45.9 us (96%)
  other arithmetic  1.04 us (2%)
    pallas_call x1, Pallas kernels, local(): step(object_slab, probe_field, offsets, counts, jnp.asarray(tables()))  45.9 us
    sub x1, other arithmetic, local(): object_slab - step(object_slab, probe_field, offsets, counts, jnp.asarray...  1.04 us

profile of v3, /device:TPU:161, one launch (start us, length us, event | category | flops | bytes accessed | tf_op | source)
XLA Modules:
  0.0 46.9 jit_solution(924281206829096638)
XLA Ops:
  0.0 0.0 copy-start
  0.0 45.9 %step.1 = f32[2,320,320]{2,1,0:T(8,128)S(1)} custom-call(f32[2,320,320]{2,1,0:T(8,128)} %obj_hbm.1, f32[2,512,512]{2,1,0:T(8,128)} %probe_hbm.1, s32[1,1,1,2]{3,2,1,0:T(1,128)} %off_hbm.1, s32[1,1,1,512,512]{4,3,2,1,0:T(8,128)} %counts_hbm.1, bf16[2,2,4,256,256]{4,3,2,1,0:T(8,128)(2,1)} %constant.2.clone.tab_hbm), custom_call_target="tpu_custom_call" | custom-call | tf_op jit(solution)/shard_map/step/pallas_call | solution.py:672
  45.9 0.0 copy-done
  45.9 1.0 %sub.3 = f32[2,320,320]{2,1,0:T(8,128)} subtract(f32[2,320,320]{2,1,0:T(8,128)S(1)} %copy-done, f32[2,320,320]{2,1,0:T(8,128)S(1)} %step.1) | non-fusion elementwise | flops 204800 | bytes 2457600 | tf_op jit(solution)/shard_map/sub | solution.py:672
Async XLA Ops:
  0.0 45.9 %copy-start = (f32[2,320,320]{2,1,0:T(8,128)S(1)}, f32[2,320,320]{2,1,0:T(8,128)}, u32[]{:S(2)}) copy-start(f32[2,320,320]{2,1,0:T(8,128)} %obj_hbm.1) | copy-start | bytes 2457604

commit v4 on v3

--- a/solution.py
+++ b/solution.py
@@ -85,8 +85,8 @@
         load(tab_hbm, tab, 3),
         load(off_hbm, off_ref, 4),
     ]
-    for c in loads:
-        c.start()
+    loads[0].start()
+    loads[4].start()
 
     barrier = pltpu.get_barrier_semaphore()
     for d in range(4):
@@ -96,7 +96,7 @@
 
     OPP = (DN, UP, RT, LF)
     CROSS = (8, 7)
-    RELAYS = {LF: (5, 3, 1), RT: (11, 13, 15)}
+    RELAYS = {LF: (3, 1, 5), RT: (13, 15, 11)}
     OWNS, GOWN = ("own0", "own1"), ("gown0", "gown1", "gown2")
     RELAYED = OWNS + ("cor0",) + GOWN
     PARTS = (slice(0, 160), slice(160, OWN))
@@ -258,6 +258,8 @@
     offs[1, 1] = jnp.where(iota((8, B), 0) == 0, uf, vf)
 
     loads[0].wait()
+    for c in loads[1:4]:
+        c.start()
     def tail(rs, n, ch):
         x = obj[ch, rs:rs + n, 256:OWN]
         return jnp.concatenate([x, x], axis=1)
@@ -413,11 +415,11 @@
 
     loads[3].wait()
     corner("outer", DN)
-    pass_on("cor0")
     for direction in (UP, DN):
         gone("inner", direction)
     go("mid", UP)
     go("mid", DN)
+    pass_on("cor0")
     corner("inner", UP)
     corner("inner", DN)
     for name in OWNS:
@@ -428,8 +430,6 @@
         [in_own[0, ch] for ch in range(2)], [in_own[1, ch] for ch in range(2)],
     )
     columns_in(INSIDE)
-    arrive("mid", UP)
-    arrive("mid", DN)
 
     groups = (0, 64, 448)
     row64 = iota((64, B), 0)
@@ -446,12 +446,6 @@
 
     for rs in groups:
         put(rs, 64, 1, *(halo(rs, lambda s, r: in_edge[s, 0, ch, r:r + 64]) for ch in range(2)))
-        m = halo(rs, lambda s, r: in_mid[s, r:r + 64])
-        put(rs, 64, 2, *(
-            jnp.where(low_half, m if ch == 0 else roll64(m), rolled_edge(rs, ch))
-            for ch in range(2)
-        ))
-
     for side in (UP, DN):
         arrive("cor%d" % side, LF)
         arrive("cor%d" % side, RT)
@@ -461,6 +455,14 @@
             [halo(rs, lambda s, r: in_cor[0, s, ch, r:r + 64]) for ch in range(2)],
             [halo(rs, lambda s, r: in_cor[1, s, ch, r:r + 64]) for ch in range(2)],
         )
+    arrive("mid", UP)
+    arrive("mid", DN)
+    for rs in groups:
+        m = halo(rs, lambda s, r: in_mid[s, r:r + 64])
+        put(rs, 64, 2, *(
+            jnp.where(low_half, m if ch == 0 else roll64(m), rolled_edge(rs, ch))
+            for ch in range(2)
+        ))
     columns_in(MARGIN)
 
     def block(ref, c, q):

time: 47.7 us -> 47.4 us (level); the launches traced: 46.9 us -> 47.2 us
  no operation moved by 1% of the time
where the time goes in v4:
time: 47.4 us; the launch traced here: 47.2 us
  Pallas kernels  46.2 us (97%)
  other arithmetic  1.04 us (2%)
    pallas_call x1, Pallas kernels, local(): step(object_slab, probe_field, offsets, counts, jnp.asarray(tables()))  46.2 us
    sub x1, other arithmetic, local(): object_slab - step(object_slab, probe_field, offsets, counts, jnp.asarray...  1.04 us

profile of v4, /device:TPU:161, one launch (start us, length us, event | category | flops | bytes accessed | tf_op | source)
XLA Modules:
  0.0 47.2 jit_solution(16836743517364381050)
XLA Ops:
  0.0 0.0 copy-start
  0.0 46.2 %step.1 = f32[2,320,320]{2,1,0:T(8,128)S(1)} custom-call(f32[2,320,320]{2,1,0:T(8,128)} %obj_hbm.1, f32[2,512,512]{2,1,0:T(8,128)} %probe_hbm.1, s32[1,1,1,2]{3,2,1,0:T(1,128)} %off_hbm.1, s32[1,1,1,512,512]{4,3,2,1,0:T(8,128)} %counts_hbm.1, bf16[2,2,4,256,256]{4,3,2,1,0:T(8,128)(2,1)} %constant.2.clone.tab_hbm), custom_call_target="tpu_custom_call" | custom-call | tf_op jit(solution)/shard_map/step/pallas_call | solution.py:674
  46.2 0.0 copy-done
  46.2 1.0 %sub.3 = f32[2,320,320]{2,1,0:T(8,128)} subtract(f32[2,320,320]{2,1,0:T(8,128)S(1)} %copy-done, f32[2,320,320]{2,1,0:T(8,128)S(1)} %step.1) | non-fusion elementwise | flops 204800 | bytes 2457600 | tf_op jit(solution)/shard_map/sub | solution.py:674
Async XLA Ops:
  0.0 46.2 %copy-start = (f32[2,320,320]{2,1,0:T(8,128)S(1)}, f32[2,320,320]{2,1,0:T(8,128)}, u32[]{:S(2)}) copy-start(f32[2,320,320]{2,1,0:T(8,128)} %obj_hbm.1) | copy-start | bytes 2457604

commit v5 on v4

--- a/solution.py
+++ b/solution.py
@@ -532,12 +532,6 @@
     go("gcor", LF)
     go("gcor", RT)
 
-    columns_out(INSIDE)
-    to_sides(INSIDE)
-    for name in GOWN:
-        go(name, LF)
-        go(name, RT)
-
     def edges(e):
         arrive("gcor", LF if e == 0 else RT)
         for side in (UP, DN):
@@ -559,6 +553,12 @@
             go("gedge%d" % e, side)
 
     for which in ("ginner", "gouter"):
+        if which == "gouter":
+            columns_out(INSIDE)
+            to_sides(INSIDE)
+            for name in GOWN:
+                go(name, LF)
+                go(name, RT)
         for e in range(2):
             @pl.when(core == (1 - e if which == "ginner" else e))
             def _():

time: 47.4 us -> 48.6 us (1.025)
  the two profiles are of different devices: /device:TPU:161 before, /device:TPU:168 now
where the time goes in v5:
time: 48.6 us; the launch traced here: 48.5 us
  Pallas kernels  47.4 us (98%)
  other arithmetic  1.04 us (2%)
    pallas_call x1, Pallas kernels, local(): step(object_slab, probe_field, offsets, counts, jnp.asarray(tables()))  47.4 us
    sub x1, other arithmetic, local(): object_slab - step(object_slab, probe_field, offsets, counts, jnp.asarray...  1.04 us

profile of v5, /device:TPU:168, one launch (start us, length us, event | category | flops | bytes accessed | tf_op | source)
XLA Modules:
  0.0 48.5 jit_solution(13967384000400181212)
XLA Ops:
  0.0 0.0 copy-start
  0.0 47.4 %step.1 = f32[2,320,320]{2,1,0:T(8,128)S(1)} custom-call(f32[2,320,320]{2,1,0:T(8,128)} %obj_hbm.1, f32[2,512,512]{2,1,0:T(8,128)} %probe_hbm.1, s32[1,1,1,2]{3,2,1,0:T(1,128)} %off_hbm.1, s32[1,1,1,512,512]{4,3,2,1,0:T(8,128)} %counts_hbm.1, bf16[2,2,4,256,256]{4,3,2,1,0:T(8,128)(2,1)} %constant.2.clone.tab_hbm), custom_call_target="tpu_custom_call" | custom-call | tf_op jit(solution)/shard_map/step/pallas_call | solution.py:674
  47.4 0.0 copy-done
  47.5 1.0 %sub.3 = f32[2,320,320]{2,1,0:T(8,128)} subtract(f32[2,320,320]{2,1,0:T(8,128)S(1)} %copy-done, f32[2,320,320]{2,1,0:T(8,128)S(1)} %step.1) | non-fusion elementwise | flops 204800 | bytes 2457600 | tf_op jit(solution)/shard_map/sub | solution.py:674
Async XLA Ops:
  0.0 47.4 %copy-start = (f32[2,320,320]{2,1,0:T(8,128)S(1)}, f32[2,320,320]{2,1,0:T(8,128)}, u32[]{:S(2)}) copy-start(f32[2,320,320]{2,1,0:T(8,128)} %obj_hbm.1) | copy-start | bytes 2457604
